TPU v7x, 32 devices: a whole 2x2x4 slice. The times are simulated.
32 devices in a mesh: row: 8 (over z, y), col: 4 (over x, core).
Axes of the slice: x: 2, y: 2, z: 4, core: 2. Of those that a mesh axis runs over, the one named last changes fastest.
Arguments:
- embeddings: bfloat16 [12288, 768], P(('row', 'col'))
- doc_order: int32 [12288], P(('row', 'col')), may hold values from 0 to 12287, each once
Outputs:
- nearest_earlier: float32 [12288], P(('row', 'col'))
Inputs may be any that keep to these rules, and one draw needn't show every extreme that they name: `doc_order`: each value 0 to 12287 appears once.
All inputs are finite; a program needn't handle non-finite values.
Results may differ from a plain program's by a relative error of at most 0.00051.
Values may be sent and summed in bfloat16 or wider, within the bound.
A program may use at most 64 MiB of HBM per device.

v0:
```python
import jax
import jax.numpy as jnp
from jax import lax
from jax.sharding import PartitionSpec as P


def normalize_rows(embeddings):
    floats = embeddings.astype(jnp.float32)
    scale = lax.rsqrt(jnp.sum(floats * floats, axis=1, keepdims=True) + 1e-06)
    return (floats * scale).astype(jnp.bfloat16)


def block_size(length):
    width = min(512, length)
    while length % width != 0:
        width = width - 1
    return width


def masked_maxima(row_units, row_orders, col_units, col_orders, running):
    length = col_units.shape[0]
    width = block_size(length)
    col_groups = col_units.reshape(length // width, width, col_units.shape[1])
    order_groups = col_orders.reshape(length // width, width)

    def one_block(current, pair):
        units_here, orders_here = pair
        scores = jnp.dot(row_units, units_here.T, preferred_element_type=jnp.float32)
        earlier = orders_here[None, :] < row_orders[:, None]
        masked = jnp.where(earlier, scores, jnp.float32(-1.0))
        return (jnp.maximum(current, jnp.max(masked, axis=1)), None)

    result, unused = lax.scan(one_block, running, (col_groups, order_groups))
    return result


def shards(embeddings, doc_order):
    unit_rows = normalize_rows(embeddings)
    own_rows = unit_rows.shape[0]
    col_count = lax.axis_size("col")
    block_rows = own_rows * col_count
    initial = jnp.full((block_rows,), -1.0, jnp.float32)
    row_units, row_orders = (
        lax.all_gather(unit_rows, "col", axis=0, tiled=True),
        lax.all_gather(doc_order, "col", axis=0, tiled=True),
    )
    best_rows = masked_maxima(
        row_units,
        row_orders,
        lax.all_gather(unit_rows, "row", axis=0, tiled=True),
        lax.all_gather(doc_order, "row", axis=0, tiled=True),
        initial,
    )
    whole_max = lax.pmax(best_rows, "col")
    own_share = lax.dynamic_slice_in_dim(whole_max, lax.axis_index("col") * own_rows, own_rows, 0)
    return jnp.maximum(own_share, jnp.float32(-1.0))


def solution(mesh):
    return jax.shard_map(
        shards,
        mesh=mesh,
        in_specs=(P(("row", "col"), None), P(("row", "col"))),
        out_specs=P(("row", "col")),
        check_vma=False,
    )
```

profile of v0, /device:TPU:0, one launch (start us, length us, event | category | flops | bytes accessed | tf_op | source)
XLA Modules:
  0.0 152.0 jit_solution(297163370144080767)
XLA Ops:
  6.5 0.0 copy-start
  6.5 0.0 all-gather.7.cloned.1.call-start
  6.5 1.3 fusion.5
  7.8 2.0 %fusion.6 = bf16[384,768]{1,0:T(8,128)(2,1)} fusion(bf16[384,768]{1,0:T(8,128)(2,1)} %param.4, f32[384]{0:T(512)S(1)} %add_rsqrt_fusion), kind=kLoop, calls=%fused_computation.11 | loop fusion | flops 884736 | bytes 1181184 | tf_op jit(solution)/shard_map/convert_element_type | solution.py:10
  9.9 0.0 all-gather.7.cloned.1.call-update
  9.9 0.0 all-gather.5.cloned.1.call-start
  9.9 0.7 all-gather.5.cloned.1.call-update
  10.7 0.0 copy-done
  10.7 27.8 %all-gather = s32[8,1,384]{2,1,0:T(1,128)S(1)} all-gather(s32[1,1,384]{2,1,0:T(1,128)S(1)} %reshape.15), channel_id=1, replica_groups=mesh['row'=8,'col'=4] {'row'}, dimensions={0}, use_global_device_ids=true | all-gather | bytes 13824 | tf_op jit(solution)/shard_map/all_gather | solution.py:51
  38.6 5.2 %all-gather.1 = s32[4,1,384]{2,1,0:T(1,128)S(1)} all-gather(s32[1,1,384]{2,1,0:T(1,128)S(1)} %reshape.15), channel_id=1, replica_groups=mesh['row'=8,'col'=4] {'col'}, dimensions={0}, use_global_device_ids=true | all-gather | bytes 7680 | tf_op jit(solution)/shard_map/all_gather | solution.py:45
  43.8 0.0 all-gather.7.cloned.1.call-done
  43.8 74.5 %all-gather.5.cloned.1.call-done = bf16[3072,768]{1,0:T(8,128)(2,1)} async-done(((bf16[384,768]{1,0:T(8,128)(2,1)}), bf16[3072,768]{1,0:T(8,128)(2,1)}) %all-gather.5.cloned.1.call-update) | async-done | bytes 4718608 | tf_op jit(solution)/shard_map/all_gather | solution.py:50
  118.3 20.4 %while.11 = (s32[]{:T(128)}, f32[1536]{0:T(1024)S(1)}, s32[6,512]{1,0:T(8,128)S(1)}, s32[1536]{0:T(1024)S(1)}, bf16[6,512,768]{2,1,0:T(8,128)(2,1)}, /*index=5*/bf16[1536,768]{1,0:T(8,128)(2,1)}, s32[]{:T(128)}, s32[]{:T(128)}) while((s32[]{:T(128)}, f32[1536]{0:T(1024)S(1)}, s32[6,512]{1,0:T(8,128)S(1)}, s32[1536]{0:T(1024)S(1)}, ...), condition=%wide.region_3.4_spmd.clone, body=%wide.region_1.3_spmd.clone.sunk | while | flops 1210320384 | bytes 3183203 | solution.py:33
  118.4 3.3 %fusion.13 = f32[1536]{0:T(1024)S(1)} fusion(bf16[1536,768]{1,0:T(8,128)(2,1)} %get-tuple-element.129, s32[1536]{0:T(1024)S(1)} %get-tuple-element.127, s32[512]{0:T(512)S(1)} %bitcast.20, bf16[6,512,768]{2,1,0:T(8,128)(2,1)} %get-tuple-element.128, s32[]{:T(128)} %get-tuple-element.116), kind=kOutput, calls=%fused_computation.2.clone.1 | convolution fusion | flops 1210317312 | bytes 3160576 | tf_op jit(solution)/shard_map/while/body/eval_jaxpr/dot_general | solution.py:28
  121.8 3.3 %fusion.13 = f32[1536]{0:T(1024)S(1)} fusion(bf16[1536,768]{1,0:T(8,128)(2,1)} %get-tuple-element.129, s32[1536]{0:T(1024)S(1)} %get-tuple-element.127, s32[512]{0:T(512)S(1)} %bitcast.20, bf16[6,512,768]{2,1,0:T(8,128)(2,1)} %get-tuple-element.128, s32[]{:T(128)} %get-tuple-element.116), kind=kOutput, calls=%fused_computation.2.clone.1 | convolution fusion | flops 1210317312 | bytes 3160576 | tf_op jit(solution)/shard_map/while/body/eval_jaxpr/dot_general | solution.py:28
  125.2 3.3 %fusion.13 = f32[1536]{0:T(1024)S(1)} fusion(bf16[1536,768]{1,0:T(8,128)(2,1)} %get-tuple-element.129, s32[1536]{0:T(1024)S(1)} %get-tuple-element.127, s32[512]{0:T(512)S(1)} %bitcast.20, bf16[6,512,768]{2,1,0:T(8,128)(2,1)} %get-tuple-element.128, s32[]{:T(128)} %get-tuple-element.116), kind=kOutput, calls=%fused_computation.2.clone.1 | convolution fusion | flops 1210317312 | bytes 3160576 | tf_op jit(solution)/shard_map/while/body/eval_jaxpr/dot_general | solution.py:28
  128.6 3.3 %fusion.13 = f32[1536]{0:T(1024)S(1)} fusion(bf16[1536,768]{1,0:T(8,128)(2,1)} %get-tuple-element.129, s32[1536]{0:T(1024)S(1)} %get-tuple-element.127, s32[512]{0:T(512)S(1)} %bitcast.20, bf16[6,512,768]{2,1,0:T(8,128)(2,1)} %get-tuple-element.128, s32[]{:T(128)} %get-tuple-element.116), kind=kOutput, calls=%fused_computation.2.clone.1 | convolution fusion | flops 1210317312 | bytes 3160576 | tf_op jit(solution)/shard_map/while/body/eval_jaxpr/dot_general | solution.py:28
  132.0 3.3 %fusion.13 = f32[1536]{0:T(1024)S(1)} fusion(bf16[1536,768]{1,0:T(8,128)(2,1)} %get-tuple-element.129, s32[1536]{0:T(1024)S(1)} %get-tuple-element.127, s32[512]{0:T(512)S(1)} %bitcast.20, bf16[6,512,768]{2,1,0:T(8,128)(2,1)} %get-tuple-element.128, s32[]{:T(128)} %get-tuple-element.116), kind=kOutput, calls=%fused_computation.2.clone.1 | convolution fusion | flops 1210317312 | bytes 3160576 | tf_op jit(solution)/shard_map/while/body/eval_jaxpr/dot_general | solution.py:28
  135.4 3.3 %fusion.13 = f32[1536]{0:T(1024)S(1)} fusion(bf16[1536,768]{1,0:T(8,128)(2,1)} %get-tuple-element.129, s32[1536]{0:T(1024)S(1)} %get-tuple-element.127, s32[512]{0:T(512)S(1)} %bitcast.20, bf16[6,512,768]{2,1,0:T(8,128)(2,1)} %get-tuple-element.128, s32[]{:T(128)} %get-tuple-element.116), kind=kOutput, calls=%fused_computation.2.clone.1 | convolution fusion | flops 1210317312 | bytes 3160576 | tf_op jit(solution)/shard_map/while/body/eval_jaxpr/dot_general | solution.py:28
  138.7 5.8 %pmax.7 = f32[1536]{0:T(1024)S(1)} all-reduce(f32[1536]{0:T(1024)S(1)} %get-tuple-element.37), channel_id=1, replica_groups=mesh['row'=8,'col'=4] {'col'}, use_global_device_ids=true, to_apply=%region_4.5 | all-reduce | flops 1536 | bytes 12288 | tf_op jit(solution)/shard_map/pmax | solution.py:54
  144.5 0.7 dynamic-slice_maximum_fusion
  (19 shorter events, 0.2 us)
Async XLA Ops:
  6.5 4.1 %copy-start = (s32[384]{0:T(512)S(1)}, s32[384]{0:T(512)}, u32[]{:S(2)}) copy-start(s32[384]{0:T(512)} %param.5) | copy-start | bytes 4612
  6.5 37.3 %all-gather.7.cloned.1.call-start = ((), (), s32[]{:S(2)}) async-start(), calls=%async_computation.1 | async-start | bytes 2949120 | tf_op jit(solution)/shard_map/all_gather | solution.py:44
  9.9 108.5 %all-gather.5.cloned.1.call-start = ((), (), s32[]{:S(2)}) async-start(), calls=%async_computation | async-start | bytes 5308416 | tf_op jit(solution)/shard_map/all_gather | solution.py:50
Sparse Core Ops, SparseCore 0:
  10.0 26.7 all-gather.6
  39.0 79.3 all-gather.4
where the time goes:
time: 152 us
  waiting for transfers between devices  75.3 us (50%)
  blocking collectives  38.8 us (26%)
  matrix products  20.1 us (13%)
  between operations  13.5 us (9%)
  other arithmetic  4.08 us (3%)
    all_gather x1, waiting for transfers between devices, shards(): lax.all_gather(unit_rows, 'row', axis=0, tiled=True)  74.5 us
    all_gather x1, blocking collectives, shards(): lax.all_gather(doc_order, 'row', axis=0, tiled=True)  27.8 us
    dot_general x6, matrix products, one_block(): jnp.dot(row_units, units_here.T, preferred_element_type=jnp.float32)  20.1 us
    pmax x1, blocking collectives, shards(): whole_max = lax.pmax(best_rows, 'col')  5.77 us
    all_gather x1, blocking collectives, shards(): lax.all_gather(doc_order, 'col', axis=0, tiled=True)  5.18 us
  transfers between devices with their start and end apart: 2, of which 1 were waited for; matrix products, arithmetic and copies ran while one was open for 0% of the time, Pallas kernels for 0%

commit v1 on v0

v1 whole, which is shorter than its diff:
```python
import functools

import jax
import jax.numpy as jnp
from jax import lax
from jax.experimental import pallas as pl
from jax.experimental.pallas import tpu as pltpu
from jax.sharding import PartitionSpec as P

MESH = pl.DeviceIdType.MESH
LANES = 128


def fast_size(rows):
    best = 1
    for size in range(1, rows + 1):
        if rows % size == 0 and size * size <= rows:
            best = size
    return best


class Layout:
    def __init__(self, rows, cols):
        self.fast = fast_size(rows)
        self.slow = rows // self.fast
        self.cores = 2 if cols % 2 == 0 else 1
        self.xs = cols // self.cores
        self.chips = self.fast * self.xs
        self.plane = self.chips * self.cores
        self.top = self.slow - 2 if self.slow > 2 else self.slow - 1
        self.down = self.slow > 2
        chips = [(f, x) for f in range(self.fast) for x in range(self.xs)]
        near = [c for c in chips if (c[0] == 0) != (c[1] == 0)]
        far = [c for c in chips if c[0] != 0 and c[1] != 0]
        self.offsets = near + far
        self.near = list(range(len(near)))
        self.far = list(range(len(near), len(near) + len(far)))
        self.peers = [
            (f, x, c)
            for f in range(self.fast)
            for x in range(self.xs)
            for c in range(self.cores)
            if (f, x, c) != (0, 0, 0)
        ]


def kernel(
    lay, n, chunks,
    emb, order, out,
    units, line, orders, line_orders, col_orders,
    row_best, col_best, plane_res, line_res, plane_in, line_in,
    ps, pr, ss, sr, ls, lr, os_, or_, los, lor, rs, rr, lrs, lrr,
):
    S, F, X, C = lay.slow, lay.fast, lay.xs, lay.cores
    rows_here = n // chunks
    r, c = lax.axis_index("row"), lax.axis_index("col")
    z, f = r // F, lax.rem(r, F)
    x, core = c // C, lax.rem(c, C)
    chip = f * X + x
    slot = chip * C + core

    def plane_id(df, dx, dc):
        return {
            "row": z * F + lax.rem(f + df, F),
            "col": lax.rem(x + dx, X) * C + lax.rem(core + dc, C),
        }

    def line_id(there):
        return {"row": there * F + f, "col": c}

    def source_chip(df, dx):
        return lax.rem(f + F - df, F) * X + lax.rem(x + X - dx, X)

    def span(which, k):
        return pl.ds(pl.multiple_of(which * n + k * rows_here, LANES), rows_here)

    def remote(src, dst, send, recv, where):
        return pltpu.make_async_remote_copy(
            src_ref=src, dst_ref=dst, send_sem=send, recv_sem=recv,
            device_id=where, device_id_type=MESH,
        )

    def plane_copy(i, k):
        part = units.at[span(slot, k)]
        return remote(part, part, ps.at[i, k], pr.at[i, k], plane_id(*lay.offsets[i], 0))

    def sibling_copy(i, k):
        src = chip if i < 0 else source_chip(*lay.offsets[i])
        part = units.at[span(src * C + core, k)]
        return remote(part, part, ss.at[i + 1, k], sr.at[i + 1, k], plane_id(0, 0, 1))

    def plane_wait(i, k):
        src = source_chip(*lay.offsets[i]) * C + core
        part = units.at[span(src, k)]
        remote(part, part, ps.at[i, k], pr.at[i, k], plane_id(*lay.offsets[i], 0)).wait_recv()

    def sibling_wait(i, k):
        src = chip if i < 0 else source_chip(*lay.offsets[i])
        part = units.at[span(src * C + lax.rem(core + 1, C), k)]
        remote(part, part, ss.at[i + 1, k], sr.at[i + 1, k], plane_id(0, 0, 1)).wait_recv()

    def line_copy(src, k, dst_slot, tag, there):
        return remote(
            src, line.at[dst_slot, pl.ds(k * rows_here, rows_here)],
            ls.at[tag, k], lr.at[dst_slot, k], line_id(there),
        )

    def own_part(k):
        return units.at[span(slot, k)]

    base = jnp.minimum(z, lay.top)
    sends_up = z < lay.top
    last = S - 1
    sends_down = (z == last) if lay.down else None
    takes_down = (z == last - 1) if lay.down else None

    def relays(w, k):
        part = line.at[w, pl.ds(k * rows_here, rows_here)]
        found = []
        if w < lay.top:
            found.append(((base >= w) & (z < lay.top), line_copy(part, k, w + 1, w, z + 1)))
        if lay.down:
            found.append(((base >= w) & (z == lay.top), line_copy(part, k, w, w, z + 1)))
        return found

    def order_copy(o):
        return remote(order, orders.at[slot], os_.at[o], or_.at[o], plane_id(*lay.peers[o]))

    def order_wait(o):
        df, dx, dc = lay.peers[o]
        src = source_chip(df, dx) * C + lax.rem(core + C - dc, C)
        remote(order, orders.at[src], os_.at[o], or_.at[o], plane_id(df, dx, dc)).wait_recv()

    def meets(src, dst):
        up = (src < dst) & ((src != lay.top) | (not lay.down))
        if lay.down:
            up = up | ((src == last) & (dst == last - 1))
        return up

    def line_order_copy(dst):
        return remote(order, line_orders.at[z], los.at[dst], lor.at[z], line_id(dst))

    barrier = pltpu.get_barrier_semaphore()
    for peer in lay.peers:
        pl.semaphore_signal(barrier, inc=1, device_id=plane_id(*peer), device_id_type=MESH)
    for dz in range(1, S):
        pl.semaphore_signal(
            barrier, inc=1, device_id=line_id(lax.rem(z + dz, S)), device_id_type=MESH
        )

    for k in range(chunks):
        floats = emb[pl.ds(k * rows_here, rows_here), :].astype(jnp.float32)
        scale = lax.rsqrt(jnp.sum(floats * floats, axis=1, keepdims=True) + 1e-06)
        units[span(slot, k), :] = (floats * scale).astype(jnp.bfloat16)

    row_best[...] = jnp.full(row_best.shape, -1.0, jnp.float32)
    col_best[...] = jnp.full(col_best.shape, -1.0, jnp.float32)
    orders[pl.ds(slot, 1)] = order[...].reshape(1, 1, n)

    def spread(which, row):
        wide = jnp.broadcast_to(row.reshape(1, n), (LANES, n))
        col_orders[which] = wide.T

    spread(lay.top + 1, order[...])
    pl.semaphore_wait(barrier, len(lay.peers) + S - 1)

    for k in range(chunks):
        pl.when(sends_up)(lambda k=k: line_copy(own_part(k), k, 1, lay.top + 1, z + 1).start())
        if lay.down:
            pl.when(sends_down)(lambda k=k: line_copy(own_part(k), k, 0, 0, z - 1).start())
        for i in lay.near:
            plane_copy(i, k).start()
        if C > 1:
            sibling_copy(-1, k).start()
    for o in range(len(lay.peers)):
        order_copy(o).start()
    for dst in range(S):
        pl.when(meets(z, dst))(lambda dst=dst: line_order_copy(dst).start())
    for i in lay.far:
        for k in range(chunks):
            plane_copy(i, k).start()

    width = C * n

    def scores(lhs, which_chip):
        rhs = units[pl.ds(pl.multiple_of(which_chip * width, LANES), width), :]
        return lax.dot_general(
            lhs, rhs, (((1,), (1,)), ((), ())), preferred_element_type=jnp.float32
        )

    def item(lhs, w, which_chip, both, first=0, count=n):
        s = scores(lhs, which_chip)
        mine = col_orders[w, first:first + count, :]
        rows_max = None
        for j in range(width // LANES):
            at = j * LANES
            part = s[:, at:at + LANES]
            core_at, lane_at = at // n, at % n
            theirs = orders[which_chip * C + core_at, :, lane_at:lane_at + LANES]
            earlier = theirs < mine
            if both:
                cand = jnp.where(earlier, part, jnp.float32(-1.0))
                rows_max = cand if rows_max is None else jnp.maximum(rows_max, cand)
                later = jnp.where(earlier, jnp.float32(-1.0), part)
            else:
                later = jnp.where(mine < theirs, part, jnp.float32(-1.0))
            down = jnp.max(later.reshape(count // 8, 8, LANES), axis=0)
            col_best[which_chip, :, at:at + LANES] = jnp.maximum(
                col_best[which_chip, :, at:at + LANES], down
            )
        if both:
            row_best[w, first:first + count, :] = jnp.maximum(
                row_best[w, first:first + count, :], rows_max
            )

    def own_item(which_chip):
        lhs = units[pl.ds(pl.multiple_of(slot * n, LANES), n), :]
        item(lhs, lay.top + 1, which_chip, False)

    def line_item(w, which_chip):
        item(line[w], w, which_chip, True)

    def valid(w):
        return takes_down if w == 0 else base >= w

    early = [w for w in ([0] if lay.down else []) + [1] if w <= lay.top]
    late = list(range(2, lay.top + 1))

    for o in range(len(lay.peers)):
        order_wait(o)
    for w in ([0] if lay.down else []) + list(range(1, lay.top + 1)):
        src = (z + 1) if w == 0 else base - w

        def take(w=w, src=src):
            remote(order, line_orders.at[src], los.at[0], lor.at[src], line_id(z)).wait_recv()
            spread(w, line_orders[src])

        pl.when(valid(w))(take)

    if C > 1:
        for k in range(chunks):
            sibling_wait(-1, k)
    own_item(chip)

    def line_wait(w, k):
        line_copy(line.at[w, pl.ds(k * rows_here, rows_here)], k, w, 0, z).wait_recv()

    def pass_on(w, k):
        pl.when(valid(w))(lambda: line_wait(w, k))
        if w > 0:
            for cond, copy in relays(w, k):
                pl.when(cond)(lambda copy=copy: copy.start())

    for k in range(chunks):
        for w in reversed(early):
            pass_on(w, k)
        for i in lay.near:
            plane_wait(i, k)
            if C > 1:
                sibling_copy(i, k).start()
    if C > 1:
        for i in lay.near:
            for k in range(chunks):
                sibling_wait(i, k)

    near_chips = [source_chip(*lay.offsets[i]) for i in lay.near]
    far_chips = [source_chip(*lay.offsets[i]) for i in lay.far]

    def sweep(ws, chips, own):
        def body(which):
            if own:
                own_item(which)
            for w in ws:
                pl.when(valid(w))(lambda w=w: line_item(w, which))

        for which in chips:
            body(which)

    work = [(early, [chip], False)] + [(early, [one], True) for one in near_chips]
    groups = [work[k::chunks] for k in range(chunks)]
    for k in range(chunks):
        for ws, chips, own in groups[k]:
            sweep(ws, chips, own)
        for w in late:
            pass_on(w, k)
        for i in lay.far:
            plane_wait(i, k)
            if C > 1:
                sibling_copy(i, k).start()
    sweep(late, [chip] + near_chips, False)
    if C > 1:
        for i in lay.far:
            for k in range(chunks):
                sibling_wait(i, k)
    sweep(early + late, far_chips, True)

    for one in range(lay.chips):
        flat = jnp.max(col_best[one], axis=0, keepdims=True)
        for core_at in range(C):
            plane_res[one * C + core_at] = flat[:, core_at * n:(core_at + 1) * n]

    for w in range(lay.top + 1):
        if w == 0 and not lay.down:
            continue

        def fold(w=w):
            line_res[w] = jnp.max(row_best[w].T, axis=0, keepdims=True)

        pl.when(valid(w))(fold)

    def result_copy(o):
        df, dx, dc = lay.peers[o]
        there = (lax.rem(f + df, F) * X + lax.rem(x + dx, X)) * C + lax.rem(core + dc, C)
        return remote(
            plane_res.at[there], plane_in.at[o], rs.at[o], rr.at[o], plane_id(df, dx, dc)
        )

    def line_result(w):
        there = z + 1 if w == 0 else base - w
        return remote(line_res.at[w], line_in.at[z], lrs.at[w], lrr.at[z], line_id(there))

    for w in range(lay.top + 1):
        if w == 0 and not lay.down:
            continue
        pl.when(valid(w))(lambda w=w: line_result(w).start())
    for o in range(len(lay.peers)):
        result_copy(o).start()

    best = jnp.maximum(plane_res[slot], jnp.float32(-1.0))
    for o in range(len(lay.peers)):
        result_copy(o).wait_recv()
        best = jnp.maximum(best, plane_in[o])
    out[...] = best
    for src in range(S):
        def gather(src=src):
            remote(
                line_res.at[0], line_in.at[src], lrs.at[0], lrr.at[src], line_id(z)
            ).wait_recv()
            out[...] = jnp.maximum(out[...], line_in[src])

        pl.when(meets(z, jnp.int32(src)))(gather)

    for k in range(chunks):
        pl.when(sends_up)(lambda k=k: line_copy(own_part(k), k, 1, lay.top + 1, z + 1).wait_send())
        if lay.down:
            pl.when(sends_down)(lambda k=k: line_copy(own_part(k), k, 0, 0, z - 1).wait_send())
        for i in range(len(lay.offsets)):
            plane_copy(i, k).wait_send()
        if C > 1:
            for i in range(-1, len(lay.offsets)):
                sibling_copy(i, k).wait_send()
        for w in range(1, lay.top + 1):
            for cond, copy in relays(w, k):
                pl.when(cond)(lambda copy=copy: copy.wait_send())
    for o in range(len(lay.peers)):
        order_copy(o).wait_send()
        result_copy(o).wait_send()
    for dst in range(S):
        pl.when(meets(z, dst))(lambda dst=dst: line_order_copy(dst).wait_send())
    for w in range(lay.top + 1):
        if w == 0 and not lay.down:
            continue
        pl.when(valid(w))(lambda w=w: line_result(w).wait_send())


def shards(lay, embeddings, doc_order):
    n, depth = embeddings.shape
    chunks = n // LANES if n % LANES == 0 else 1
    dma = pltpu.SemaphoreType.DMA
    near, peers, top, S = len(lay.offsets), len(lay.peers), lay.top, lay.slow
    found = pl.pallas_call(
        functools.partial(kernel, lay, n, chunks),
        out_shape=jax.ShapeDtypeStruct((1, n), jnp.float32),
        in_specs=[pl.BlockSpec(memory_space=pltpu.VMEM)] * 2,
        out_specs=pl.BlockSpec(memory_space=pltpu.VMEM),
        scratch_shapes=[
            pltpu.VMEM((lay.plane * n, depth), jnp.bfloat16),
            pltpu.VMEM((top + 1, n, depth), jnp.bfloat16),
            pltpu.VMEM((lay.plane, 1, n), jnp.int32),
            pltpu.VMEM((S, 1, n), jnp.int32),
            pltpu.VMEM((top + 2, n, LANES), jnp.int32),
            pltpu.VMEM((top + 1, n, LANES), jnp.float32),
            pltpu.VMEM((lay.chips, 8, lay.cores * n), jnp.float32),
            pltpu.VMEM((lay.plane, 1, n), jnp.float32),
            pltpu.VMEM((top + 1, 1, n), jnp.float32),
            pltpu.VMEM((peers, 1, n), jnp.float32),
            pltpu.VMEM((S, 1, n), jnp.float32),
            dma((near, chunks)), dma((near, chunks)),
            dma((near + 1, chunks)), dma((near + 1, chunks)),
            dma((top + 2, chunks)), dma((top + 1, chunks)),
            dma((peers,)), dma((peers,)),
            dma((S,)), dma((S,)),
            dma((peers,)), dma((peers,)),
            dma((top + 1,)), dma((S,)),
        ],
        compiler_params=pltpu.CompilerParams(
            collective_id=0, has_side_effects=True, vmem_limit_bytes=60 * 1024 * 1024
        ),
    )(embeddings, doc_order.reshape(1, n))
    return found.reshape(n)


def solution(mesh):
    lay = Layout(mesh.shape["row"], mesh.shape["col"])
    return jax.shard_map(
        functools.partial(shards, lay),
        mesh=mesh,
        in_specs=(P(("row", "col"), None), P(("row", "col"))),
        out_specs=P(("row", "col")),
        check_vma=False,
    )
```

time: 152 us -> 62.1 us (0.41)
  waiting for transfers between devices: 75.3 us -> 0 us
  Pallas kernels: 0 us -> 59.4 us
  blocking collectives: 38.8 us -> 0 us
  matrix products: 20.1 us -> 0 us
  between operations: 13.5 us -> 0.01 us
  other arithmetic: 4.08 us -> 1.28 us
    all_gather x2 -> x0, waiting for transfers between devices: 74.6 us -> none  [the longest x1 74.5 us: shards(): lax.all_gather(unit_rows, 'row', axis=0, tiled=True)]
    pallas_call x0 -> x1, Pallas kernels: none -> 59.4 us  [shards(): pl.pallas_call(functools.partial(kernel, lay, n, chunks), out_shape=jax.S...]
    all_gather x2 -> x0, blocking collectives: 33 us -> none  [the longest x1 27.8 us: shards(): lax.all_gather(doc_order, 'row', axis=0, tiled=True)]
    dot_general x6 -> x0, matrix products: 20.1 us -> none  [one_block(): jnp.dot(row_units, units_here.T, preferred_element_type=jnp.float32)]
    pmax x1 -> x0, blocking collectives: 5.77 us -> none  [shards(): whole_max = lax.pmax(best_rows, 'col')]
    convert_element_type x1 -> x0, other arithmetic: 2.04 us -> none  [normalize_rows(): return (floats * scale).astype(jnp.bfloat16)]
  transfers between devices with their start and end apart: 2 -> 0, of which waited for: 1 -> 0; matrix products, arithmetic and copies ran while one was open for 0% -> 0% of each run, Pallas kernels for 0% -> 0%
where the time goes in v1:
time: 62.1 us; the launch traced here: 61.9 us
  Pallas kernels  59.4 us (96%)
  other arithmetic  1.28 us (2%)
  local copies, waits for them, and re-layouts  1.24 us (2%)
    pallas_call x1, Pallas kernels, shards(): pl.pallas_call(functools.partial(kernel, lay, n, chunks), out_shape=jax.S...  59.4 us
    pallas_call x1, other arithmetic, shards(): pl.pallas_call(functools.partial(kernel, lay, n, chunks), out_shape=jax.S...  1.28 us
    reshape x1, local copies, waits for them, and re-layouts, shards(): doc_order.reshape(1, n)  1.24 us

profile of v1, /device:TPU:0, one launch (start us, length us, event | category | flops | bytes accessed | tf_op | source)
XLA Modules:
  0.0 61.9 jit_solution(14333326992907366039)
XLA Ops:
  0.0 1.2 %reshape.6.order = s32[1,384]{1,0:T(1,128)} reshape(s32[384]{0:T(512)} %param.3) | data formatting | bytes 3072 | tf_op jit(solution)/shard_map/reshape | solution.py:399
  1.2 59.4 %shard_map.28 = f32[1,384]{1,0:T(1,128)} custom-call(bf16[384,768]{1,0:T(8,128)(2,1)} %emb.1, s32[1,384]{1,0:T(1,128)} %reshape.6.order), custom_call_target="tpu_custom_call" | custom-call | tf_op jit(solution)/shard_map/pallas_call | solution.py:371
  60.6 1.3 %reduce = f32[384]{0:T(512)} reduce(f32[1,384]{1,0:T(1,128)} %shard_map.28, f32[]{:T(128)} %constant), dimensions={0}, to_apply=%pallas_call.3.reduce_sub_computation | reduce | bytes 3076 | tf_op jit(solution)/shard_map/pallas_call | solution.py:371

commit v2 on v1

--- a/solution.py
+++ b/solution.py
@@ -9,6 +9,8 @@
 
 MESH = pl.DeviceIdType.MESH
 LANES = 128
+PIECE = 64
+GROUP = 128
 
 
 def fast_size(rows):
@@ -48,11 +50,12 @@
     lay, n, chunks,
     emb, order, out,
     units, line, orders, line_orders, col_orders,
-    row_best, col_best, plane_res, line_res, plane_in, line_in,
+    row_best, col_best, plane_res, line_res, plane_in, line_in, line_best,
     ps, pr, ss, sr, ls, lr, os_, or_, los, lor, rs, rr, lrs, lrr,
 ):
     S, F, X, C = lay.slow, lay.fast, lay.xs, lay.cores
     rows_here = n // chunks
+    align = PIECE if rows_here % PIECE == 0 else rows_here
     r, c = lax.axis_index("row"), lax.axis_index("col")
     z, f = r // F, lax.rem(r, F)
     x, core = c // C, lax.rem(c, C)
@@ -72,7 +75,7 @@
         return lax.rem(f + F - df, F) * X + lax.rem(x + X - dx, X)
 
     def span(which, k):
-        return pl.ds(pl.multiple_of(which * n + k * rows_here, LANES), rows_here)
+        return pl.ds(pl.multiple_of(which * n + k * rows_here, align), rows_here)
 
     def remote(src, dst, send, recv, where):
         return pltpu.make_async_remote_copy(
@@ -83,6 +86,12 @@
     def plane_copy(i, k):
         part = units.at[span(slot, k)]
         return remote(part, part, ps.at[i, k], pr.at[i, k], plane_id(*lay.offsets[i], 0))
+
+    def relay_copy(i, k):
+        df, dx = lay.offsets[i]
+        src, step = ((0, dx), (df, 0)) if k % 2 == 0 else ((df, 0), (0, dx))
+        part = units.at[span(source_chip(*src) * C + core, k)]
+        return remote(part, part, ps.at[i, k], pr.at[i, k], plane_id(*step, 0))
 
     def sibling_copy(i, k):
         src = chip if i < 0 else source_chip(*lay.offsets[i])
@@ -124,12 +133,12 @@
         return found
 
     def order_copy(o):
-        return remote(order, orders.at[slot], os_.at[o], or_.at[o], plane_id(*lay.peers[o]))
+        return remote(orders.at[slot], orders.at[slot], os_.at[o], or_.at[o], plane_id(*lay.peers[o]))
 
     def order_wait(o):
         df, dx, dc = lay.peers[o]
         src = source_chip(df, dx) * C + lax.rem(core + C - dc, C)
-        remote(order, orders.at[src], os_.at[o], or_.at[o], plane_id(df, dx, dc)).wait_recv()
+        remote(orders.at[slot], orders.at[src], os_.at[o], or_.at[o], plane_id(df, dx, dc)).wait_recv()
 
     def meets(src, dst):
         up = (src < dst) & ((src != lay.top) | (not lay.down))
@@ -138,7 +147,7 @@
         return up
 
     def line_order_copy(dst):
-        return remote(order, line_orders.at[z], los.at[dst], lor.at[z], line_id(dst))
+        return remote(orders.at[slot], line_orders.at[z], los.at[dst], lor.at[z], line_id(dst))
 
     barrier = pltpu.get_barrier_semaphore()
     for peer in lay.peers:
@@ -148,37 +157,39 @@
             barrier, inc=1, device_id=line_id(lax.rem(z + dz, S)), device_id_type=MESH
         )
 
-    for k in range(chunks):
+    orders[pl.ds(slot, 1)] = order[...].reshape(1, 1, n)
+
+    def spread(which, row):
+        wide = jnp.broadcast_to(row.reshape(1, n), (LANES, n))
+        col_orders[which] = wide.T
+
+    def normalize(k):
         floats = emb[pl.ds(k * rows_here, rows_here), :].astype(jnp.float32)
         scale = lax.rsqrt(jnp.sum(floats * floats, axis=1, keepdims=True) + 1e-06)
         units[span(slot, k), :] = (floats * scale).astype(jnp.bfloat16)
 
-    row_best[...] = jnp.full(row_best.shape, -1.0, jnp.float32)
-    col_best[...] = jnp.full(col_best.shape, -1.0, jnp.float32)
-    orders[pl.ds(slot, 1)] = order[...].reshape(1, 1, n)
-
-    def spread(which, row):
-        wide = jnp.broadcast_to(row.reshape(1, n), (LANES, n))
-        col_orders[which] = wide.T
-
-    spread(lay.top + 1, order[...])
-    pl.semaphore_wait(barrier, len(lay.peers) + S - 1)
-
-    for k in range(chunks):
-        pl.when(sends_up)(lambda k=k: line_copy(own_part(k), k, 1, lay.top + 1, z + 1).start())
+    def send_own(k):
+        pl.when(sends_up)(lambda: line_copy(own_part(k), k, 1, lay.top + 1, z + 1).start())
         if lay.down:
-            pl.when(sends_down)(lambda k=k: line_copy(own_part(k), k, 0, 0, z - 1).start())
+            pl.when(sends_down)(lambda: line_copy(own_part(k), k, 0, 0, z - 1).start())
         for i in lay.near:
             plane_copy(i, k).start()
         if C > 1:
             sibling_copy(-1, k).start()
+
+    for k in range(chunks):
+        normalize(k)
+    pl.semaphore_wait(barrier, len(lay.peers) + S - 1)
+    for dst in range(S):
+        pl.when(meets(z, dst))(lambda dst=dst: line_order_copy(dst).start())
     for o in range(len(lay.peers)):
         order_copy(o).start()
-    for dst in range(S):
-        pl.when(meets(z, dst))(lambda dst=dst: line_order_copy(dst).start())
-    for i in lay.far:
-        for k in range(chunks):
-            plane_copy(i, k).start()
+    for k in range(chunks):
+        send_own(k)
+
+    row_best[...] = jnp.full(row_best.shape, -1.0, jnp.float32)
+    col_best[...] = jnp.full(col_best.shape, -1.0, jnp.float32)
+    spread(lay.top + 1, order[...].reshape(1, n))
 
     width = C * n
 
@@ -232,7 +243,7 @@
         src = (z + 1) if w == 0 else base - w
 
         def take(w=w, src=src):
-            remote(order, line_orders.at[src], los.at[0], lor.at[src], line_id(z)).wait_recv()
+            remote(orders.at[slot], line_orders.at[src], los.at[0], lor.at[src], line_id(z)).wait_recv()
             spread(w, line_orders[src])
 
         pl.when(valid(w))(take)
@@ -251,48 +262,106 @@
             for cond, copy in relays(w, k):
                 pl.when(cond)(lambda copy=copy: copy.start())
 
+    def chips_of(places):
+        def at(j):
+            if places == "near":
+                by_x = j < X - 1
+                df = jnp.where(by_x, 0, j - (X - 2))
+                dx = jnp.where(by_x, j + 1, 0)
+            elif places == "far":
+                df, dx = 1 + j // max(X - 1, 1), 1 + lax.rem(j, max(X - 1, 1))
+            elif places == "self":
+                df, dx = 0, 0
+            else:
+                df, dx = j // X, lax.rem(j, X)
+            return source_chip(df, dx)
+
+        count = {"near": F + X - 2, "far": (F - 1) * (X - 1), "self": 1, "all": F * X}
+        return count[places], at
+
+    def loop(places, body):
+        count, at = chips_of(places)
+
+        def step(j, carry):
+            body(at(j))
+            return carry
+
+        if count:
+            lax.fori_loop(0, count, step, 0)
+
+    def own_sweep(places):
+        loop(places, own_item)
+
+    def line_sweep(w, places):
+        pl.when(valid(w))(lambda: loop(places, lambda one: line_item(w, one)))
+
+    def late_sweep(w, g):
+        first = g * group
+
+        def body(one):
+            item(line[w, first:first + group, :], w, one, True, first, group)
+
+        pl.when(valid(w))(lambda: loop("all", body))
+
+    group = GROUP if n % GROUP == 0 else n
+    groups = n // group
+    per = chunks // groups if chunks % groups == 0 else chunks
+    if chunks % groups != 0:
+        group, groups = n, 1
+
     for k in range(chunks):
         for w in reversed(early):
             pass_on(w, k)
         for i in lay.near:
             plane_wait(i, k)
-            if C > 1:
+        for i in lay.far:
+            relay_copy(i, k).start()
+        if C > 1:
+            for i in lay.near:
                 sibling_copy(i, k).start()
-    if C > 1:
-        for i in lay.near:
-            for k in range(chunks):
-                sibling_wait(i, k)
-
-    near_chips = [source_chip(*lay.offsets[i]) for i in lay.near]
-    far_chips = [source_chip(*lay.offsets[i]) for i in lay.far]
-
-    def sweep(ws, chips, own):
-        def body(which):
-            if own:
-                own_item(which)
-            for w in ws:
-                pl.when(valid(w))(lambda w=w: line_item(w, which))
-
-        for which in chips:
-            body(which)
-
-    work = [(early, [chip], False)] + [(early, [one], True) for one in near_chips]
-    groups = [work[k::chunks] for k in range(chunks)]
+
+    work = [lambda: own_sweep("near")]
+    for w in reversed(early):
+        work.append(lambda w=w: line_sweep(w, "near"))
+        work.append(lambda w=w: line_sweep(w, "self"))
+    far_work = [lambda: own_sweep("far")]
+    for w in reversed(early):
+        far_work.append(lambda w=w: line_sweep(w, "far"))
+
+    half = chunks // 2
+    far_pieces = [list(range(2 * k, min(2 * k + 2, chunks))) for k in range(chunks)]
+    if half == 0:
+        far_pieces = [list(range(chunks))]
+    pending = []
     for k in range(chunks):
-        for ws, chips, own in groups[k]:
-            sweep(ws, chips, own)
         for w in late:
             pass_on(w, k)
-        for i in lay.far:
-            plane_wait(i, k)
+        for j in far_pieces[k]:
+            for i in lay.far:
+                plane_wait(i, j)
+                if C > 1:
+                    sibling_copy(i, j).start()
+        if k == 0:
             if C > 1:
-                sibling_copy(i, k).start()
-    sweep(late, [chip] + near_chips, False)
-    if C > 1:
-        for i in lay.far:
-            for k in range(chunks):
-                sibling_wait(i, k)
-    sweep(early + late, far_chips, True)
+                for i in lay.near:
+                    for j in range(chunks):
+                        sibling_wait(i, j)
+            pending += work
+        if k == min(half, chunks - 1):
+            if C > 1:
+                for i in lay.far:
+                    for j in range(chunks):
+                        sibling_wait(i, j)
+            pending += far_work
+        if k == min(half, chunks - 1):
+            for g in range((k + 1) // per):
+                pending += [lambda w=w, g=g: late_sweep(w, g) for w in late]
+        elif k > half and (k + 1) % per == 0:
+            pending += [lambda w=w, g=(k + 1) // per - 1: late_sweep(w, g) for w in late]
+        take = len(pending) if k == chunks - 1 else 2
+        for run in pending[:take]:
+            run()
+        pending = pending[take:]
 
     for one in range(lay.chips):
         flat = jnp.max(col_best[one], axis=0, keepdims=True)
@@ -330,22 +399,25 @@
     for o in range(len(lay.peers)):
         result_copy(o).wait_recv()
         best = jnp.maximum(best, plane_in[o])
-    out[...] = best
+    line_best[...] = best.reshape(1, n)
     for src in range(S):
         def gather(src=src):
             remote(
                 line_res.at[0], line_in.at[src], lrs.at[0], lrr.at[src], line_id(z)
             ).wait_recv()
-            out[...] = jnp.maximum(out[...], line_in[src])
+            line_best[...] = jnp.maximum(line_best[...], line_in[src])
 
         pl.when(meets(z, jnp.int32(src)))(gather)
 
+    out[...] = line_best[...].reshape(n)
     for k in range(chunks):
         pl.when(sends_up)(lambda k=k: line_copy(own_part(k), k, 1, lay.top + 1, z + 1).wait_send())
         if lay.down:
             pl.when(sends_down)(lambda k=k: line_copy(own_part(k), k, 0, 0, z - 1).wait_send())
-        for i in range(len(lay.offsets)):
+        for i in lay.near:
             plane_copy(i, k).wait_send()
+        for i in lay.far:
+            relay_copy(i, k).wait_send()
         if C > 1:
             for i in range(-1, len(lay.offsets)):
                 sibling_copy(i, k).wait_send()
@@ -365,12 +437,12 @@
 
 def shards(lay, embeddings, doc_order):
     n, depth = embeddings.shape
-    chunks = n // LANES if n % LANES == 0 else 1
+    chunks = n // PIECE if n % PIECE == 0 else 1
     dma = pltpu.SemaphoreType.DMA
     near, peers, top, S = len(lay.offsets), len(lay.peers), lay.top, lay.slow
     found = pl.pallas_call(
         functools.partial(kernel, lay, n, chunks),
-        out_shape=jax.ShapeDtypeStruct((1, n), jnp.float32),
+        out_shape=jax.ShapeDtypeStruct((n,), jnp.float32),
         in_specs=[pl.BlockSpec(memory_space=pltpu.VMEM)] * 2,
         out_specs=pl.BlockSpec(memory_space=pltpu.VMEM),
         scratch_shapes=[
@@ -385,6 +457,7 @@
             pltpu.VMEM((top + 1, 1, n), jnp.float32),
             pltpu.VMEM((peers, 1, n), jnp.float32),
             pltpu.VMEM((S, 1, n), jnp.float32),
+            pltpu.VMEM((1, n), jnp.float32),
             dma((near, chunks)), dma((near, chunks)),
             dma((near + 1, chunks)), dma((near + 1, chunks)),
             dma((top + 2, chunks)), dma((top + 1, chunks)),
@@ -396,8 +469,8 @@
         compiler_params=pltpu.CompilerParams(
             collective_id=0, has_side_effects=True, vmem_limit_bytes=60 * 1024 * 1024
         ),
-    )(embeddings, doc_order.reshape(1, n))
-    return found.reshape(n)
+    )(embeddings, doc_order)
+    return found
 
 
 def solution(mesh):

time: 62.1 us -> 50.3 us (0.81)
  Pallas kernels: 59.4 us -> 48.9 us
  other arithmetic: 1.28 us -> 0 us
    pallas_call x1, Pallas kernels: 59.4 us -> 48.9 us  [shards(): pl.pallas_call(functools.partial(kernel, lay, n, chunks), out_shape=jax.S...]
    pallas_call x1 -> x0, other arithmetic: 1.28 us -> none  [shards(): pl.pallas_call(functools.partial(kernel, lay, n, chunks), out_shape=jax.S...]
    unnamed x0 -> x1, local copies, waits for them, and re-layouts: none -> 1.26 us
    reshape x1 -> x0, local copies, waits for them, and re-layouts: 1.24 us -> none  [shards(): doc_order.reshape(1, n)]
where the time goes in v2:
time: 50.3 us; the launch traced here: 50.2 us
  Pallas kernels  48.9 us (97%)
  local copies, waits for them, and re-layouts  1.26 us (3%)
    pallas_call x1, Pallas kernels, shards(): pl.pallas_call(functools.partial(kernel, lay, n, chunks), out_shape=jax.S...  48.9 us
    unnamed x1, local copies, waits for them, and re-layouts  1.26 us

profile of v2, /device:TPU:0, one launch (start us, length us, event | category | flops | bytes accessed | tf_op | source)
XLA Modules:
  0.0 50.2 jit_solution(2118541816858129441)
XLA Ops:
  0.0 48.9 %shard_map.28 = f32[384]{0:T(512)} custom-call(bf16[384,768]{1,0:T(8,128)(2,1)} %emb.1, s32[384]{0:T(512)} %order.1), custom_call_target="tpu_custom_call" | custom-call | tf_op jit(solution)/shard_map/pallas_call | solution.py:443
  48.9 1.3 %copy.4 = f32[384]{0:T(512)} copy(f32[384]{0:T(512)} %shard_map.28) | data formatting | bytes 3072

commit v3 on v2

--- a/solution.py
+++ b/solution.py
@@ -193,19 +193,16 @@
 
     width = C * n
 
-    def scores(lhs, which_chip):
-        rhs = units[pl.ds(pl.multiple_of(which_chip * width, LANES), width), :]
-        return lax.dot_general(
+    def item(lhs, w, first_chip, both, first=0, count=n, wide=1):
+        rhs = units[pl.ds(pl.multiple_of(first_chip * width, LANES), wide * width), :]
+        s = lax.dot_general(
             lhs, rhs, (((1,), (1,)), ((), ())), preferred_element_type=jnp.float32
         )
-
-    def item(lhs, w, which_chip, both, first=0, count=n):
-        s = scores(lhs, which_chip)
         mine = col_orders[w, first:first + count, :]
         rows_max = None
-        for j in range(width // LANES):
-            at = j * LANES
-            part = s[:, at:at + LANES]
+        for j in range(wide * width // LANES):
+            part = s[:, j * LANES:(j + 1) * LANES]
+            which_chip, at = first_chip + j * LANES // width, j * LANES % width
             core_at, lane_at = at // n, at % n
             theirs = orders[which_chip * C + core_at, :, lane_at:lane_at + LANES]
             earlier = theirs < mine
@@ -270,13 +267,13 @@
                 dx = jnp.where(by_x, j + 1, 0)
             elif places == "far":
                 df, dx = 1 + j // max(X - 1, 1), 1 + lax.rem(j, max(X - 1, 1))
-            elif places == "self":
-                df, dx = 0, 0
+            elif places == "home":
+                df, dx = jnp.where(j < X, 0, j - (X - 1)), jnp.where(j < X, j, 0)
             else:
                 df, dx = j // X, lax.rem(j, X)
             return source_chip(df, dx)
 
-        count = {"near": F + X - 2, "far": (F - 1) * (X - 1), "self": 1, "all": F * X}
+        count = {"near": F + X - 2, "far": (F - 1) * (X - 1), "home": F + X - 1, "all": F * X}
         return count[places], at
 
     def loop(places, body):
@@ -295,19 +292,16 @@
     def line_sweep(w, places):
         pl.when(valid(w))(lambda: loop(places, lambda one: line_item(w, one)))
 
-    def late_sweep(w, g):
-        first = g * group
-
-        def body(one):
-            item(line[w, first:first + group, :], w, one, True, first, group)
-
-        pl.when(valid(w))(lambda: loop("all", body))
-
-    group = GROUP if n % GROUP == 0 else n
-    groups = n // group
-    per = chunks // groups if chunks % groups == 0 else chunks
-    if chunks % groups != 0:
-        group, groups = n, 1
+    wide = next(m for m in (4, 3, 2, 1) if lay.chips % m == 0)
+
+    def late_sweep(w, first, count):
+        def body(j, carry):
+            item(line[w, first:first + count, :], w, j * wide, True, first, count, wide)
+            return carry
+
+        @pl.when(valid(w))
+        def run():
+            lax.fori_loop(0, lay.chips // wide, body, 0)
 
     for k in range(chunks):
         for w in reversed(early):
@@ -320,19 +314,23 @@
             for i in lay.near:
                 sibling_copy(i, k).start()
 
-    work = [lambda: own_sweep("near")]
-    for w in reversed(early):
-        work.append(lambda w=w: line_sweep(w, "near"))
-        work.append(lambda w=w: line_sweep(w, "self"))
-    far_work = [lambda: own_sweep("far")]
-    for w in reversed(early):
-        far_work.append(lambda w=w: line_sweep(w, "far"))
-
-    half = chunks // 2
+    def when_at(sixths):
+        return min(chunks * sixths // 6, chunks - 1)
+
+    plan = [[] for _ in range(chunks)]
+    plan[when_at(0)].append(lambda: own_sweep("near"))
+    for place, sixths in (("home", 1), ("far", 3)):
+        for j, w in enumerate(reversed(early)):
+            plan[when_at(sixths + j)].append(lambda w=w, place=place: line_sweep(w, place))
+    plan[when_at(3)].append(lambda: own_sweep("far"))
+    split = n * 2 // 3 if chunks % 6 == 0 and n * 2 // 3 % GROUP == 0 else 0
+    for w in late:
+        if split:
+            plan[when_at(4)].append(lambda w=w: late_sweep(w, 0, split))
+        plan[chunks - 1].append(lambda w=w: late_sweep(w, split, n - split))
     far_pieces = [list(range(2 * k, min(2 * k + 2, chunks))) for k in range(chunks)]
-    if half == 0:
-        far_pieces = [list(range(chunks))]
-    pending = []
+    if chunks == 1:
+        far_pieces = [[0]]
     for k in range(chunks):
         for w in late:
             pass_on(w, k)
@@ -341,27 +339,16 @@
                 plane_wait(i, j)
                 if C > 1:
                     sibling_copy(i, j).start()
-        if k == 0:
-            if C > 1:
-                for i in lay.near:
-                    for j in range(chunks):
-                        sibling_wait(i, j)
-            pending += work
-        if k == min(half, chunks - 1):
-            if C > 1:
-                for i in lay.far:
-                    for j in range(chunks):
-                        sibling_wait(i, j)
-            pending += far_work
-        if k == min(half, chunks - 1):
-            for g in range((k + 1) // per):
-                pending += [lambda w=w, g=g: late_sweep(w, g) for w in late]
-        elif k > half and (k + 1) % per == 0:
-            pending += [lambda w=w, g=(k + 1) // per - 1: late_sweep(w, g) for w in late]
-        take = len(pending) if k == chunks - 1 else 2
-        for run in pending[:take]:
+        if C > 1 and k == 0:
+            for i in lay.near:
+                for j in range(chunks):
+                    sibling_wait(i, j)
+        if C > 1 and k == when_at(3):
+            for i in lay.far:
+                for j in range(chunks):
+                    sibling_wait(i, j)
+        for run in plan[k]:
             run()
-        pending = pending[take:]
 
     for one in range(lay.chips):
         flat = jnp.max(col_best[one], axis=0, keepdims=True)

time: 50.3 us -> 46.8 us (0.930)
  Pallas kernels: 48.9 us -> 45.4 us
    pallas_call x1, Pallas kernels: 48.9 us -> 45.4 us  [shards(): pl.pallas_call(functools.partial(kernel, lay, n, chunks), out_shape=jax.S...]
where the time goes in v3:
time: 46.8 us; the launch traced here: 46.7 us
  Pallas kernels  45.4 us (97%)
  local copies, waits for them, and re-layouts  1.26 us (3%)
    pallas_call x1, Pallas kernels, shards(): pl.pallas_call(functools.partial(kernel, lay, n, chunks), out_shape=jax.S...  45.4 us
    unnamed x1, local copies, waits for them, and re-layouts  1.26 us

profile of v3, /device:TPU:0, one launch (start us, length us, event | category | flops | bytes accessed | tf_op | source)
XLA Modules:
  0.0 46.7 jit_solution(2107184672955592577)
XLA Ops:
  0.0 45.4 %shard_map.28 = f32[384]{0:T(512)} custom-call(bf16[384,768]{1,0:T(8,128)(2,1)} %emb.1, s32[384]{0:T(512)} %order.1), custom_call_target="tpu_custom_call" | custom-call | tf_op jit(solution)/shard_map/pallas_call | solution.py:430
  45.4 1.3 %copy.4 = f32[384]{0:T(512)} copy(f32[384]{0:T(512)} %shard_map.28) | data formatting | bytes 3072

commit v4 on v3

--- a/solution.py
+++ b/solution.py
@@ -51,7 +51,7 @@
     emb, order, out,
     units, line, orders, line_orders, col_orders,
     row_best, col_best, plane_res, line_res, plane_in, line_in, line_best,
-    ps, pr, ss, sr, ls, lr, os_, or_, los, lor, rs, rr, lrs, lrr,
+    ps, pr, ss, sr, ls, lr, os_, or_, los, lor, oss, osr, rs, rr, lrs, lrr,
 ):
     S, F, X, C = lay.slow, lay.fast, lay.xs, lay.cores
     rows_here = n // chunks
@@ -132,13 +132,23 @@
             found.append(((base >= w) & (z == lay.top), line_copy(part, k, w, w, z + 1)))
         return found
 
-    def order_copy(o):
-        return remote(orders.at[slot], orders.at[slot], os_.at[o], or_.at[o], plane_id(*lay.peers[o]))
-
-    def order_wait(o):
-        df, dx, dc = lay.peers[o]
-        src = source_chip(df, dx) * C + lax.rem(core + C - dc, C)
-        remote(orders.at[slot], orders.at[src], os_.at[o], or_.at[o], plane_id(df, dx, dc)).wait_recv()
+    def order_send(src, i, where):
+        return remote(orders.at[src], orders.at[src], os_.at[i], or_.at[i], where)
+
+    def order_copy(i):
+        return order_send(slot, i, plane_id(*lay.offsets[i], 0))
+
+    def order_relay(i):
+        df, dx = lay.offsets[i]
+        return order_send(source_chip(0, dx) * C + core, i, plane_id(df, 0, 0))
+
+    def order_wait(i):
+        order_send(source_chip(*lay.offsets[i]) * C + core, i, plane_id(0, 0, 1)).wait_recv()
+
+    def order_across(i, side):
+        src = chip if i < 0 else source_chip(*lay.offsets[i])
+        part = orders.at[src * C + lax.rem(core + side, C)]
+        return remote(part, part, oss.at[i + 1], osr.at[i + 1], plane_id(0, 0, 1))
 
     def meets(src, dst):
         up = (src < dst) & ((src != lay.top) | (not lay.down))
@@ -146,15 +156,28 @@
             up = up | ((src == last) & (dst == last - 1))
         return up
 
-    def line_order_copy(dst):
-        return remote(orders.at[slot], line_orders.at[z], los.at[dst], lor.at[z], line_id(dst))
+    def line_order_copy(part, src, tag, there):
+        return remote(part, line_orders.at[src], los.at[tag], lor.at[src], line_id(there))
+
+    def own_order(there):
+        return line_order_copy(orders.at[slot], z, 0, there)
+
+    def order_up(w):
+        return line_order_copy(line_orders.at[base - w], base - w, w, z + 1)
+
+    def goes_on(w):
+        return (base >= w) & (z < last) & (lay.down | (z < lay.top))
 
     barrier = pltpu.get_barrier_semaphore()
-    for peer in lay.peers:
-        pl.semaphore_signal(barrier, inc=1, device_id=plane_id(*peer), device_id_type=MESH)
-    for dz in range(1, S):
-        pl.semaphore_signal(
-            barrier, inc=1, device_id=line_id(lax.rem(z + dz, S)), device_id_type=MESH
+    steps = [(*lay.offsets[i], 0) for i in lay.near] + ([(0, 0, 1)] if C > 1 else [])
+    sides = ((z > 0, z - 1), (z < last, z + 1))
+    for step in steps:
+        pl.semaphore_signal(barrier, inc=1, device_id=plane_id(*step), device_id_type=MESH)
+    for there, which in sides:
+        pl.when(there)(
+            lambda which=which: pl.semaphore_signal(
+                barrier, inc=1, device_id=line_id(which), device_id_type=MESH
+            )
         )
 
     orders[pl.ds(slot, 1)] = order[...].reshape(1, 1, n)
@@ -179,11 +202,15 @@
 
     for k in range(chunks):
         normalize(k)
-    pl.semaphore_wait(barrier, len(lay.peers) + S - 1)
-    for dst in range(S):
-        pl.when(meets(z, dst))(lambda dst=dst: line_order_copy(dst).start())
-    for o in range(len(lay.peers)):
-        order_copy(o).start()
+    lines = jnp.minimum(z, 1) + jnp.minimum(last - z, 1)
+    pl.semaphore_wait(barrier, len(steps) + lines)
+    pl.when(sends_up)(lambda: own_order(z + 1).start())
+    if lay.down:
+        pl.when(sends_down)(lambda: own_order(z - 1).start())
+    for i in lay.near:
+        order_copy(i).start()
+    if C > 1:
+        order_across(-1, 0).start()
     for k in range(chunks):
         send_own(k)
 
@@ -234,26 +261,34 @@
     early = [w for w in ([0] if lay.down else []) + [1] if w <= lay.top]
     late = list(range(2, lay.top + 1))
 
-    for o in range(len(lay.peers)):
-        order_wait(o)
-    for w in ([0] if lay.down else []) + list(range(1, lay.top + 1)):
+    def take_order(w):
         src = (z + 1) if w == 0 else base - w
-
-        def take(w=w, src=src):
-            remote(orders.at[slot], line_orders.at[src], los.at[0], lor.at[src], line_id(z)).wait_recv()
-            spread(w, line_orders[src])
-
-        pl.when(valid(w))(take)
-
+        line_order_copy(line_orders.at[src], src, 0, z).wait_recv()
+        if w > 0:
+            pl.when(goes_on(w))(lambda: order_up(w).start())
+        spread(w, line_orders[src])
+
+    for i in lay.near:
+        order_wait(i)
+        if C > 1:
+            order_across(i, 0).start()
+    for i in lay.far:
+        order_relay(i).start()
     if C > 1:
+        order_across(-1, 1).wait_recv()
         for k in range(chunks):
             sibling_wait(-1, k)
     own_item(chip)
+    if C > 1:
+        for i in lay.near:
+            order_across(i, 1).wait_recv()
 
     def line_wait(w, k):
         line_copy(line.at[w, pl.ds(k * rows_here, rows_here)], k, w, 0, z).wait_recv()
 
     def pass_on(w, k):
+        if k == 0:
+            pl.when(valid(w))(lambda: take_order(w))
         pl.when(valid(w))(lambda: line_wait(w, k))
         if w > 0:
             for cond, copy in relays(w, k):
@@ -267,13 +302,13 @@
                 dx = jnp.where(by_x, j + 1, 0)
             elif places == "far":
                 df, dx = 1 + j // max(X - 1, 1), 1 + lax.rem(j, max(X - 1, 1))
-            elif places == "home":
-                df, dx = jnp.where(j < X, 0, j - (X - 1)), jnp.where(j < X, j, 0)
+            elif places == "self":
+                df, dx = 0, 0
             else:
                 df, dx = j // X, lax.rem(j, X)
             return source_chip(df, dx)
 
-        count = {"near": F + X - 2, "far": (F - 1) * (X - 1), "home": F + X - 1, "all": F * X}
+        count = {"near": F + X - 2, "far": (F - 1) * (X - 1), "self": 1, "all": F * X}
         return count[places], at
 
     def loop(places, body):
@@ -294,12 +329,12 @@
 
     wide = next(m for m in (4, 3, 2, 1) if lay.chips % m == 0)
 
-    def late_sweep(w, first, count):
+    def late_sweep(w, first, count, here):
         def body(j, carry):
             item(line[w, first:first + count, :], w, j * wide, True, first, count, wide)
             return carry
 
-        @pl.when(valid(w))
+        @pl.when(valid(w) & here)
         def run():
             lax.fori_loop(0, lay.chips // wide, body, 0)
 
@@ -319,15 +354,26 @@
 
     plan = [[] for _ in range(chunks)]
     plan[when_at(0)].append(lambda: own_sweep("near"))
-    for place, sixths in (("home", 1), ("far", 3)):
-        for j, w in enumerate(reversed(early)):
-            plan[when_at(sixths + j)].append(lambda w=w, place=place: line_sweep(w, place))
-    plan[when_at(3)].append(lambda: own_sweep("far"))
+    for j, w in enumerate(reversed(early)):
+        plan[when_at(1 + 2 * j)].append(lambda w=w: line_sweep(w, "near"))
+        plan[when_at(2)].append(lambda w=w: line_sweep(w, "self"))
+    plan[when_at(4)].append(lambda: own_sweep("far"))
+    for j, w in enumerate(reversed(early)):
+        plan[when_at(4 + j)].append(lambda w=w: line_sweep(w, "far"))
     split = n * 2 // 3 if chunks % 6 == 0 and n * 2 // 3 % GROUP == 0 else 0
+    relaying = z == lay.top
     for w in late:
         if split:
-            plan[when_at(4)].append(lambda w=w: late_sweep(w, 0, split))
-        plan[chunks - 1].append(lambda w=w: late_sweep(w, split, n - split))
+            plan[(chunks * 2 + 2) // 3 - 1].append(
+                lambda w=w: late_sweep(w, 0, split, jnp.logical_not(relaying))
+            )
+            plan[chunks - 1].append(lambda w=w: late_sweep(w, 0, n, relaying))
+            plan[chunks - 1].append(
+                lambda w=w: late_sweep(w, split, n - split, jnp.logical_not(relaying))
+            )
+        else:
+            plan[chunks - 1].append(lambda w=w: late_sweep(w, 0, n, z >= 0))
+    far_at = (chunks * 2 + 2) // 3 - 1
     far_pieces = [list(range(2 * k, min(2 * k + 2, chunks))) for k in range(chunks)]
     if chunks == 1:
         far_pieces = [[0]]
@@ -343,7 +389,15 @@
             for i in lay.near:
                 for j in range(chunks):
                     sibling_wait(i, j)
-        if C > 1 and k == when_at(3):
+        if k == far_at:
+            for i in lay.far:
+                order_wait(i)
+                if C > 1:
+                    order_across(i, 0).start()
+            if C > 1:
+                for i in lay.far:
+                    order_across(i, 1).wait_recv()
+        if C > 1 and k == far_at:
             for i in lay.far:
                 for j in range(chunks):
                     sibling_wait(i, j)
@@ -412,10 +466,19 @@
             for cond, copy in relays(w, k):
                 pl.when(cond)(lambda copy=copy: copy.wait_send())
     for o in range(len(lay.peers)):
-        order_copy(o).wait_send()
         result_copy(o).wait_send()
-    for dst in range(S):
-        pl.when(meets(z, dst))(lambda dst=dst: line_order_copy(dst).wait_send())
+    for i in lay.near:
+        order_copy(i).wait_send()
+    for i in lay.far:
+        order_relay(i).wait_send()
+    if C > 1:
+        for i in range(-1, len(lay.offsets)):
+            order_across(i, 0).wait_send()
+    pl.when(sends_up)(lambda: own_order(z + 1).wait_send())
+    if lay.down:
+        pl.when(sends_down)(lambda: own_order(z - 1).wait_send())
+    for w in range(1, lay.top + 1):
+        pl.when(goes_on(w))(lambda w=w: order_up(w).wait_send())
     for w in range(lay.top + 1):
         if w == 0 and not lay.down:
             continue
@@ -426,7 +489,7 @@
     n, depth = embeddings.shape
     chunks = n // PIECE if n % PIECE == 0 else 1
     dma = pltpu.SemaphoreType.DMA
-    near, peers, top, S = len(lay.offsets), len(lay.peers), lay.top, lay.slow
+    near, peers, top, S = max(len(lay.offsets), 1), max(len(lay.peers), 1), lay.top, lay.slow
     found = pl.pallas_call(
         functools.partial(kernel, lay, n, chunks),
         out_shape=jax.ShapeDtypeStruct((n,), jnp.float32),
@@ -448,8 +511,9 @@
             dma((near, chunks)), dma((near, chunks)),
             dma((near + 1, chunks)), dma((near + 1, chunks)),
             dma((top + 2, chunks)), dma((top + 1, chunks)),
-            dma((peers,)), dma((peers,)),
-            dma((S,)), dma((S,)),
+            dma((near,)), dma((near,)),
+            dma((top + 1,)), dma((S,)),
+            dma((near + 1,)), dma((near + 1,)),
             dma((peers,)), dma((peers,)),
             dma((top + 1,)), dma((S,)),
         ],

time: 46.8 us -> 46.1 us (0.985)
  Pallas kernels: 45.4 us -> 44.7 us
    pallas_call x1, Pallas kernels: 45.4 us -> 44.7 us  [shards(): pl.pallas_call(functools.partial(kernel, lay, n, chunks), out_shape=jax.S...]
where the time goes in v4:
time: 46.1 us; the launch traced here: 45.9 us
  Pallas kernels  44.7 us (97%)
  local copies, waits for them, and re-layouts  1.26 us (3%)
    pallas_call x1, Pallas kernels, shards(): pl.pallas_call(functools.partial(kernel, lay, n, chunks), out_shape=jax.S...  44.7 us
    unnamed x1, local copies, waits for them, and re-layouts  1.26 us

profile of v4, /device:TPU:0, one launch (start us, length us, event | category | flops | bytes accessed | tf_op | source)
XLA Modules:
  0.0 45.9 jit_solution(1360271853117559468)
XLA Ops:
  0.0 44.7 %shard_map.28 = f32[384]{0:T(512)} custom-call(bf16[384,768]{1,0:T(8,128)(2,1)} %emb.1, s32[384]{0:T(512)} %order.1), custom_call_target="tpu_custom_call" | custom-call | tf_op jit(solution)/shard_map/pallas_call | solution.py:493
  44.7 1.3 %copy.4 = f32[384]{0:T(512)} copy(f32[384]{0:T(512)} %shard_map.28) | data formatting | bytes 3072

commit v5 on v4

--- a/solution.py
+++ b/solution.py
@@ -349,6 +349,16 @@
             for i in lay.near:
                 sibling_copy(i, k).start()
 
+    def line_result(w):
+        there = z + 1 if w == 0 else base - w
+        return remote(line_res.at[w], line_in.at[z], lrs.at[w], lrr.at[z], line_id(there))
+
+    def give_back(w):
+        @pl.when(valid(w))
+        def fold():
+            line_res[w] = jnp.max(row_best[w].T, axis=0, keepdims=True)
+            line_result(w).start()
+
     def when_at(sixths):
         return min(chunks * sixths // 6, chunks - 1)
 
@@ -362,6 +372,8 @@
         plan[when_at(4 + j)].append(lambda w=w: line_sweep(w, "far"))
     split = n * 2 // 3 if chunks % 6 == 0 and n * 2 // 3 % GROUP == 0 else 0
     relaying = z == lay.top
+    for w in reversed(early):
+        plan[chunks - 1].append(lambda w=w: give_back(w))
     for w in late:
         if split:
             plan[(chunks * 2 + 2) // 3 - 1].append(
@@ -404,19 +416,13 @@
         for run in plan[k]:
             run()
 
+    for w in late:
+        give_back(w)
+
     for one in range(lay.chips):
         flat = jnp.max(col_best[one], axis=0, keepdims=True)
         for core_at in range(C):
             plane_res[one * C + core_at] = flat[:, core_at * n:(core_at + 1) * n]
-
-    for w in range(lay.top + 1):
-        if w == 0 and not lay.down:
-            continue
-
-        def fold(w=w):
-            line_res[w] = jnp.max(row_best[w].T, axis=0, keepdims=True)
-
-        pl.when(valid(w))(fold)
 
     def result_copy(o):
         df, dx, dc = lay.peers[o]
@@ -425,14 +431,6 @@
             plane_res.at[there], plane_in.at[o], rs.at[o], rr.at[o], plane_id(df, dx, dc)
         )
 
-    def line_result(w):
-        there = z + 1 if w == 0 else base - w
-        return remote(line_res.at[w], line_in.at[z], lrs.at[w], lrr.at[z], line_id(there))
-
-    for w in range(lay.top + 1):
-        if w == 0 and not lay.down:
-            continue
-        pl.when(valid(w))(lambda w=w: line_result(w).start())
     for o in range(len(lay.peers)):
         result_copy(o).start()
 

time: 46.1 us -> 46.1 us (level)
  no operation moved by 1% of the time
where the time goes in v5:
time: 46.1 us; the launch traced here: 45.9 us
  Pallas kernels  44.6 us (97%)
  local copies, waits for them, and re-layouts  1.26 us (3%)
    pallas_call x1, Pallas kernels, shards(): pl.pallas_call(functools.partial(kernel, lay, n, chunks), out_shape=jax.S...  44.6 us
    unnamed x1, local copies, waits for them, and re-layouts  1.26 us

profile of v5, /device:TPU:0, one launch (start us, length us, event | category | flops | bytes accessed | tf_op | source)
XLA Modules:
  0.0 45.9 jit_solution(8619153619026612643)
XLA Ops:
  0.0 44.6 %shard_map.28 = f32[384]{0:T(512)} custom-call(bf16[384,768]{1,0:T(8,128)(2,1)} %emb.1, s32[384]{0:T(512)} %order.1), custom_call_target="tpu_custom_call" | custom-call | tf_op jit(solution)/shard_map/pallas_call | solution.py:491
  44.6 1.3 %copy.4 = f32[384]{0:T(512)} copy(f32[384]{0:T(512)} %shard_map.28) | data formatting | bytes 3072
